TPU v7x, 256 devices: a whole 4x4x8 slice. The times are simulated.
256 devices in a mesh: row: 32 (over z, y_hi, core), col: 8 (over x, y_lo).
Axes of the slice: x: 4, y: 4 (y_hi: 2, y_lo: 2; y = y_hi * 2 + y_lo), z: 8, core: 2. Of those that a mesh axis runs over, the one named last changes fastest.
Arguments:
- states: bfloat16 [768, 8192], P(None, 'col'), may hold values from -6 to 6
- norm_gain: float32 [8192], P('col'), may hold values from 0.25 to 1.75
- gate_weight: bfloat16 [8192, 28672], P('col', 'row'), may hold values from -0.0625 to 0.0625
- up_weight: bfloat16 [8192, 28672], P('col', 'row'), may hold values from -0.0625 to 0.0625
Outputs:
- near_tiles: float32 [32, 16, 896, 896], P('row', 'col')
- far_tiles: float32 [32, 896, 896], P('row', 'col')
All inputs are finite; a program needn't handle non-finite values.
Results may differ from a plain program's by a relative error of at most 0.0071.
Values may be sent and summed in bfloat16 or wider, within the bound.
No kernel may reach another device: no remote copies, remote signals or barrier semaphores. Data moves between devices by JAX's collectives and lax.ppermute only.
A program may use at most 64 MiB of HBM per device.

v0:
```python
import functools

import jax
import jax.numpy as jnp
from jax import lax
from jax.experimental import pallas as pl
from jax.experimental.pallas import tpu as pltpu
from jax.sharding import Mesh
from jax.sharding import PartitionSpec as P


D = 8192
ROW = ("z", "yh", "k")
COL = ("x", "yl")
PLANE = ("x", "yh", "yl")
SLOTS_VMEM = 4 * 2**20
TILE_VMEM = 16 * 2**20


def exchange(pieces, axes):
    return lax.all_to_all(pieces, axes, split_axis=0, concat_axis=0, tiled=True)


def copy_for_each(shard, axes):
    return exchange(jnp.broadcast_to(shard, (lax.axis_size(axes), *shard.shape)), axes)


def passed_along(shard, axis, by):
    devices = lax.axis_size(axis)
    return lax.ppermute(shard, axis, [(i, (i + by) % devices) for i in range(devices)])


def cross(left, right):
    return lax.dot_general(
        left, right, (((0,), (0,)), ((), ())), preferred_element_type=jnp.float32
    )


def slots_kernel(*refs):
    ahead, out_ref, sems = refs[:5], refs[5], refs[6]
    yh = lax.axis_index("yh")

    def copy(j, slot):
        return pltpu.make_async_copy(ahead[j], out_ref.at[slot], sems.at[slot])

    for j in range(4):
        copy(j, 4 * j).start()
        copy(j + 1, 4 * j + 3).start()
        for slot in (4 * j + 1, 4 * j + 2):

            @pl.when(yh == 0)
            def _():
                copy(j + 1, slot).start()

            @pl.when(yh != 0)
            def _():
                copy(j, slot).start()

    for slot in range(16):
        copy(0, slot).wait()


def slots(ahead):
    return pl.pallas_call(
        slots_kernel,
        in_specs=[pl.BlockSpec(memory_space=pltpu.VMEM)] * 5,
        out_specs=pl.BlockSpec(memory_space=pltpu.HBM),
        out_shape=pltpu.HBM((16, *ahead[0].shape), ahead[0].dtype),
        scratch_shapes=[pltpu.SemaphoreType.DMA((16,))],
        cost_estimate=pl.CostEstimate(
            flops=16 * ahead[0].size, bytes_accessed=42 * ahead[0].size, transcendentals=0
        ),
        compiler_params=pltpu.CompilerParams(vmem_limit_bytes=SLOTS_VMEM),
        name="slots",
    )(*ahead)


def tile_kernel(place, left_ref, right_ref, *refs):
    out_ref, rows_ref, sems = refs[-3:]
    chunks, rows, _ = rows_ref.shape
    scale = 1.0 / right_ref.shape[0]

    def copy(i):
        return pltpu.make_async_copy(
            rows_ref.at[i], out_ref.at[place, pl.ds(i * rows, rows)], sems.at[i]
        )

    for i in range(chunks):
        left = left_ref[i * rows : (i + 1) * rows, :]
        product = jnp.dot(left, right_ref[...], preferred_element_type=jnp.float32)
        rows_ref[i] = product * scale
        copy(i).start()
    for i in range(chunks):
        copy(i).wait()


def tile_into(place, keys_t, partner, tiles=None, chunks=4):
    width, count = keys_t.shape
    rows = width // chunks
    in_specs = [pl.BlockSpec(memory_space=pltpu.VMEM)] * 2
    args = [keys_t, partner]
    if tiles is not None:
        in_specs.append(pl.BlockSpec(memory_space=pltpu.HBM))
        args.append(tiles)
    return pl.pallas_call(
        functools.partial(tile_kernel, place),
        in_specs=in_specs,
        out_specs=pl.BlockSpec(memory_space=pltpu.HBM),
        out_shape=pltpu.HBM((2, width, width), jnp.float32),
        scratch_shapes=[
            pltpu.VMEM((chunks, rows, width), jnp.float32),
            pltpu.SemaphoreType.DMA((chunks,)),
        ],
        input_output_aliases={} if tiles is None else {2: 0},
        cost_estimate=pl.CostEstimate(
            flops=2 * width * width * count,
            bytes_accessed=4 * width * count + 4 * width * width,
            transcendentals=0,
        ),
        compiler_params=pltpu.CompilerParams(vmem_limit_bytes=TILE_VMEM),
        name="tile",
    )(*args)


def fetch_kernel(states_in, gate_in, up_in, squares_ref, states_ref, gate_ref, up_ref, sems):
    pairs = ((states_in, states_ref), (gate_in, gate_ref), (up_in, up_ref))
    copies = [pltpu.make_async_copy(a, b, sems.at[i]) for i, (a, b) in enumerate(pairs)]
    for copy in copies:
        copy.start()
    copies[0].wait()
    wide = states_ref[...].astype(jnp.float32)
    total = jnp.sum(wide * wide, axis=1, keepdims=True)
    total = jnp.broadcast_to(total, (wide.shape[0], 128)).T
    squares_ref[...] = jnp.broadcast_to(total[None, :1], squares_ref.shape)
    for copy in copies[1:]:
        copy.wait()


def fetched(states, gate_weight, up_weight, copies):
    arrays = (states, gate_weight, up_weight)
    count, depth = states.shape
    return pl.pallas_call(
        fetch_kernel,
        in_specs=[pl.BlockSpec(memory_space=pltpu.HBM)] * 3,
        out_specs=[pl.BlockSpec(memory_space=pltpu.VMEM)] * 4,
        out_shape=[pltpu.VMEM((copies, 1, count), jnp.float32)]
        + [pltpu.VMEM(array.shape, array.dtype) for array in arrays],
        scratch_shapes=[pltpu.SemaphoreType.DMA((3,))],
        cost_estimate=pl.CostEstimate(
            flops=2 * count * depth,
            bytes_accessed=2 * sum(array.size for array in arrays),
            transcendentals=0,
        ),
        compiler_params=pltpu.CompilerParams(vmem_limit_bytes=58 * 2**20),
        name="fetch",
    )(*arrays)


def sums_kernel(states_ref, squares_ref, gain_ref, gate_ref, up_ref, out_ref):
    width = gate_ref.shape[1]
    squares = jnp.sum(squares_ref[...], axis=0)
    inverse = lax.rsqrt(squares / D + 1e-05)
    inverse = jnp.broadcast_to(inverse, (128, inverse.shape[1])).T[:, :1]
    rows = states_ref.shape[0] // 2
    for i in range(2):
        at = slice(i * rows, (i + 1) * rows)
        normed = states_ref[at, :].astype(jnp.float32) * inverse[at, :] * gain_ref[...]
        normed = normed.astype(jnp.bfloat16)
        for j, weight in enumerate((gate_ref, up_ref)):
            part = jnp.dot(normed, weight[...], preferred_element_type=jnp.float32)
            out_ref[at, j * width : (j + 1) * width] = part.astype(jnp.bfloat16)


def partial_sums(states, squares, norm_gain, gate_weight, up_weight):
    count, depth = states.shape
    width = gate_weight.shape[1]
    return pl.pallas_call(
        sums_kernel,
        in_specs=[pl.BlockSpec(memory_space=pltpu.VMEM)] * 5,
        out_specs=pl.BlockSpec(memory_space=pltpu.VMEM),
        out_shape=jax.ShapeDtypeStruct((count, 2 * width), jnp.bfloat16),
        cost_estimate=pl.CostEstimate(
            flops=4 * count * depth * width,
            bytes_accessed=2 * (count * depth + 2 * depth * width + 2 * count * width),
            transcendentals=0,
        ),
        compiler_params=pltpu.CompilerParams(vmem_limit_bytes=24 * 2**20),
        name="sums",
    )(states, squares, norm_gain[None, :], gate_weight, up_weight)


def on_device(states, norm_gain, gate_weight, up_weight):
    n_col = lax.axis_size(COL)
    column = lax.axis_index(COL)
    yh, yl, core = lax.axis_index("yh"), lax.axis_index("yl"), lax.axis_index("k")
    count = states.shape[0]
    width = gate_weight.shape[1]
    share = count // n_col
    scale = 1.0 / count

    squares, *arrays = fetched(states, gate_weight, up_weight, n_col)
    parts = partial_sums(arrays[0], exchange(squares, COL), norm_gain, *arrays[1:])
    parts = exchange(parts.reshape(n_col, share, 2 * width), COL)
    summed = jnp.sum(parts.astype(jnp.float32), axis=0)
    own = (jax.nn.silu(summed[:, :width]) * summed[:, width:]).astype(jnp.bfloat16)

    ahead = [own]
    two = passed_along(own, "z", -2)
    one = passed_along(two, "z", 1)
    three = passed_along(two, "z", -1)
    keys = copy_for_each(own, COL).reshape(count, width)
    ahead = [own, one, two, three, passed_along(three, "z", -1)]
    outgoing, keys = lax.optimization_barrier((slots(ahead), keys))
    returned = exchange(outgoing, PLANE)

    slab = width // n_col
    own_cols = lax.dynamic_slice_in_dim(keys, column * slab, slab, 1)
    their_cols = passed_along(own_cols, "z", 4)
    their_far = (cross(their_cols, keys) * scale).astype(jnp.bfloat16)
    far_tiles = passed_along(their_far, "z", 4).astype(jnp.float32)[None]
    returned, far_tiles, keys_t = lax.optimization_barrier((returned, far_tiles, keys.T))

    returned = returned.reshape(4, 2, 2, share, width)
    near = jnp.bitwise_xor(yh, yl)
    swap = jnp.where(core == 0, 1 - near, near)
    second = lax.dynamic_index_in_dim(returned, swap, 1, keepdims=False)
    second = passed_along(second.reshape(count, width), "k", 1)
    first = lax.dynamic_index_in_dim(returned, near, 1, keepdims=False)
    tiles = tile_into(0, keys_t, first.reshape(count, width))
    near_tiles = tile_into(1, keys_t, second, tiles)[None]
    return (near_tiles, far_tiles)


def solution(mesh):
    torus = Mesh(mesh.devices.reshape(8, 2, 2, 4, 2), ("z", "yh", "k", "x", "yl"))
    in_specs = (P(None, COL), P(COL), P(COL, ROW), P(COL, ROW))
    out_specs = (P(ROW, COL, None, None), P(ROW, COL, None))

    return jax.shard_map(
        on_device, mesh=torus, in_specs=in_specs, out_specs=out_specs, check_vma=False
    )
```

profile of v0, /device:TPU:1, one launch (start us, length us, event | category | flops | bytes accessed | tf_op | source)
XLA Modules:
  0.0 133.5 jit_solution(8569135064442985465)
XLA Ops:
  0.6 0.0 copy-start
  0.6 2.6 %fetch.1 = (f32[8,1,768]{2,1,0:T(1,128)S(1)}, bf16[768,1024]{1,0:T(8,128)(2,1)S(1)}, bf16[1024,896]{1,0:T(8,128)(2,1)S(1)}, bf16[1024,896]{1,0:T(8,128)(2,1)S(1)}) custom-call(bf16[768,1024]{1,0:T(8,128)(2,1)} %states_in.1, bf16[1024,896]{1,0:T(8,128)(2,1)} %gate_in.1, bf16[1024,896]{1,0:T(8,128)(2,1)} %up_in.1), custom_call_target="tpu_custom_call" | custom-call | flops 1572864 | bytes 5242880 | tf_op jit(solution)/shard_map/fetch/pallas_call | solution.py:142
  3.2 10.7 %all_to_all.20.squares_ref = f32[8,1,768]{2,1,0:T(1,128)S(1)} all-to-all(f32[8,1,768]{2,1,0:T(1,128)S(1)} %get-tuple-element.12), channel_id=1, replica_groups=mesh['z'=8,'yh'=2,'k'=2,'x'=4,'yl'=2] {'x','yl'}, dimensions={0} | all-to-all | bytes 49152 | tf_op jit(solution)/shard_map/all_to_all | solution.py:21
  13.9 0.0 copy-done
  13.9 3.8 %sums.1 = bf16[768,1792]{1,0:T(8,128)(2,1)S(1)} custom-call(bf16[768,1024]{1,0:T(8,128)(2,1)S(1)} %get-tuple-element.11.states_ref, f32[8,1,768]{2,1,0:T(1,128)S(1)} %all_to_all.20.squares_ref, f32[1,1024]{1,0:T(1,128)S(1)} %bitcast.21, bf16[1024,896]{1,0:T(8,128)(2,1)S(1)} %get-tuple-element.13.gate_ref, bf16[1024,896]{1,0:T(8,128)(2,1)S(1)} %get-tuple-element.14.up_ref), custom_call_target="tpu_custom_call" | custom-call | flops 2818572288 | bytes 7995392 | tf_op jit(solution)/shard_map/sums/pallas_call | solution.py:177
  17.7 33.6 %all_to_all.21 = bf16[8,96,1792]{2,1,0:T(8,128)(2,1)S(1)} all-to-all(bf16[8,96,1792]{2,1,0:T(8,128)(2,1)S(1)} %bitcast.20), channel_id=1, replica_groups=mesh['z'=8,'yh'=2,'k'=2,'x'=4,'yl'=2] {'x','yl'}, dimensions={0} | all-to-all | bytes 5505024 | tf_op jit(solution)/shard_map/all_to_all | solution.py:21
  51.3 0.4 convert_reduce_fusion
  51.7 0.1 fusion.1.refs_0_
  51.8 1.2 broadcast_in_dim.16
  53.0 3.6 %all-to-all-start.2 = ((bf16[8,96,896]{2,1,0:T(8,128)(2,1)}), bf16[8,96,896]{2,1,0:T(8,128)(2,1)S(1)}, u32[]{:S(2)}, u32[]{:S(2)}) async-start(bf16[8,96,896]{2,1,0:T(8,128)(2,1)} %broadcast_in_dim.16), calls=%async_computation.2 | async-start | bytes 2752512 | tf_op jit(solution)/shard_map/all_to_all | solution.py:21
  56.6 6.1 %collective-permute-start = (bf16[96,896]{1,0:T(8,128)(2,1)S(1)}, bf16[96,896]{1,0:T(8,128)(2,1)S(1)}, u32[]{:S(2)}, u32[]{:S(2)}) collective-permute-start(bf16[96,896]{1,0:T(8,128)(2,1)S(1)} %fusion.1.refs_0_), channel_id=1, source_target_pairs={{0,192},{32,224},{64,0},{96,32},{128,64},{160,96},{192,128},{224,1... | collective-permute-start | bytes 516104 | tf_op jit(solution)/shard_map/ppermute | solution.py:30
  62.7 2.5 %collective-permute-done.refs_2_ = bf16[96,896]{1,0:T(8,128)(2,1)S(1)} collective-permute-done((bf16[96,896]{1,0:T(8,128)(2,1)S(1)}, bf16[96,896]{1,0:T(8,128)(2,1)S(1)}, u32[]{:S(2)}, u32[]{:S(2)}) %collective-permute-start) | collective-permute-done | bytes 172064 | tf_op jit(solution)/shard_map/ppermute | solution.py:30
  65.2 5.3 %collective-permute-start.2 = (bf16[96,896]{1,0:T(8,128)(2,1)S(1)}, bf16[96,896]{1,0:T(8,128)(2,1)S(1)}, u32[]{:S(2)}, u32[]{:S(2)}) collective-permute-start(bf16[96,896]{1,0:T(8,128)(2,1)S(1)} %collective-permute-done.refs_2_), channel_id=1, source_target_pairs={{0,224},{32,0},{64,32},{96,64},{128,96},{160,128},{192,160},{224,1... | collective-permute-start | bytes 516104 | tf_op jit(solution)/shard_map/ppermute | solution.py:30
  70.5 0.0 collective-permute-start.1
  70.5 2.5 %collective-permute-done.2.refs_3_ = bf16[96,896]{1,0:T(8,128)(2,1)S(1)} collective-permute-done((bf16[96,896]{1,0:T(8,128)(2,1)S(1)}, bf16[96,896]{1,0:T(8,128)(2,1)S(1)}, u32[]{:S(2)}, u32[]{:S(2)}) %collective-permute-start.2) | collective-permute-done | bytes 172064 | tf_op jit(solution)/shard_map/ppermute | solution.py:30
  73.0 3.3 %collective-permute-start.3 = (bf16[96,896]{1,0:T(8,128)(2,1)S(1)}, bf16[96,896]{1,0:T(8,128)(2,1)S(1)}, u32[]{:S(2)}, u32[]{:S(2)}) collective-permute-start(bf16[96,896]{1,0:T(8,128)(2,1)S(1)} %collective-permute-done.2.refs_3_), channel_id=1, source_target_pairs={{0,224},{32,0},{64,32},{96,64},{128,96},{160,128},{192,160},{224,1... | collective-permute-start | bytes 516104 | tf_op jit(solution)/shard_map/ppermute | solution.py:30
  76.3 0.0 collective-permute-done.1.refs_1_
  76.3 3.5 %collective-permute-done.3.refs_4_ = bf16[96,896]{1,0:T(8,128)(2,1)S(1)} collective-permute-done((bf16[96,896]{1,0:T(8,128)(2,1)S(1)}, bf16[96,896]{1,0:T(8,128)(2,1)S(1)}, u32[]{:S(2)}, u32[]{:S(2)}) %collective-permute-start.3) | collective-permute-done | bytes 172064 | tf_op jit(solution)/shard_map/ppermute | solution.py:30
  79.7 1.7 %slots.1 = bf16[16,96,896]{2,1,0:T(8,128)(2,1)} custom-call(bf16[96,896]{1,0:T(8,128)(2,1)S(1)} %fusion.1.refs_0_, bf16[96,896]{1,0:T(8,128)(2,1)S(1)} %collective-permute-done.1.refs_1_, bf16[96,896]{1,0:T(8,128)(2,1)S(1)} %collective-permute-done.refs_2_, bf16[96,896]{1,0:T(8,128)(2,1)S(1)} %collective-permute-done.2.refs_3_, ...), custom_call_target="tpu_custom_call" | custom-call | flops 1376256 | bytes 3612672 | tf_op jit(solution)/shard_map/slots/pallas_call | solution.py:64
  81.4 0.0 all-to-all-done.2
  81.4 7.0 %all-to-all-start.3 = ((bf16[16,96,896]{2,1,0:T(8,128)(2,1)}), bf16[16,96,896]{2,1,0:T(8,128)(2,1)}, u32[]{:S(2)}, u32[]{:S(2)}) async-start(bf16[16,96,896]{2,1,0:T(8,128)(2,1)} %slots.1), calls=%async_computation.3 | async-start | bytes 5505024 | tf_op jit(solution)/shard_map/all_to_all | solution.py:21
  88.4 0.1 constant_dynamic-slice_fusion.2
  88.5 2.5 %collective-permute-start.4 = (bf16[768,112]{1,0:T(8,128)(2,1)S(1)}, bf16[768,112]{1,0:T(8,128)(2,1)S(1)}, u32[]{:S(2)}, u32[]{:S(2)}) collective-permute-start(bf16[768,112]{1,0:T(8,128)(2,1)S(1)} %constant_dynamic-slice_fusion.2), channel_id=1, source_target_pairs={{0,128},{32,160},{64,192},{96,224},{128,0},{160,32},{192,64},{224,... | collective-permute-start | bytes 516104 | tf_op jit(solution)/shard_map/ppermute | solution.py:30
  91.0 8.0 %collective-permute-done.4 = bf16[768,112]{1,0:T(8,128)(2,1)S(1)} collective-permute-done((bf16[768,112]{1,0:T(8,128)(2,1)S(1)}, bf16[768,112]{1,0:T(8,128)(2,1)S(1)}, u32[]{:S(2)}, u32[]{:S(2)}) %collective-permute-start.4) | collective-permute-done | bytes 172064 | tf_op jit(solution)/shard_map/ppermute | solution.py:30
  99.0 0.4 fusion
  99.4 2.1 %collective-permute-start.5 = (bf16[112,896]{1,0:T(8,128)(2,1)S(1)}, bf16[112,896]{1,0:T(8,128)(2,1)S(1)}, u32[]{:S(2)}, u32[]{:S(2)}) collective-permute-start(bf16[112,896]{1,0:T(8,128)(2,1)S(1)} %fusion), channel_id=1, source_target_pairs={{0,128},{32,160},{64,192},{96,224},{128,0},{160,32},{192,64},{224,... | collective-permute-start | bytes 602120 | tf_op jit(solution)/shard_map/ppermute | solution.py:30
  101.5 0.9 copy.10
  102.3 6.6 %collective-permute-done.5 = bf16[112,896]{1,0:T(8,128)(2,1)S(1)} collective-permute-done((bf16[112,896]{1,0:T(8,128)(2,1)S(1)}, bf16[112,896]{1,0:T(8,128)(2,1)S(1)}, u32[]{:S(2)}, u32[]{:S(2)}) %collective-permute-start.5) | collective-permute-done | bytes 200736 | tf_op jit(solution)/shard_map/ppermute | solution.py:30
  109.0 0.8 bitcast_convert_fusion
  109.7 7.5 %all-to-all-done.3 = bf16[16,96,896]{2,1,0:T(8,128)(2,1)} async-done(((bf16[16,96,896]{2,1,0:T(8,128)(2,1)}), bf16[16,96,896]{2,1,0:T(8,128)(2,1)}, u32[]{:S(2)}, u32[]{:S(2)}) %all-to-all-start.3) | async-done | bytes 2752544 | tf_op jit(solution)/shard_map/all_to_all | solution.py:21
  117.2 2.0 %constant_dynamic-slice_fusion = (bf16[4,1,2,96,896]{4,3,2,1,0:T(8,128)(2,1)S(1)}, bf16[4,1,2,96,896]{4,3,2,1,0:T(8,128)(2,1)S(1)}) fusion(bf16[4,2,2,96,896]{4,3,2,1,0:T(8,128)(2,1)} %bitcast.5, s32[]{:T(128)S(6)} %select_n.17, s32[]{:T(128)S(6)} %select_n.16), kind=kLoop, calls=%fused_computation.6 | loop fusion | bytes 5505032 | tf_op jit(solution)/shard_map/jit(dynamic_index_in_dim)/dynamic_slice | solution.py:228
  119.2 8.9 %collective-permute-start.6 = (bf16[768,896]{1,0:T(8,128)(2,1)S(1)}, bf16[768,896]{1,0:T(8,128)(2,1)S(1)}, u32[]{:S(2)}, u32[]{:S(2)}) collective-permute-start(bf16[768,896]{1,0:T(8,128)(2,1)S(1)} %bitcast.26), channel_id=1, source_target_pairs={{0,8},{8,0},{1,9},{9,1},{2,10},{10,2},{3,11},{11,3},{4,12},{12,4},... | collective-permute-start | bytes 4128776 | tf_op jit(solution)/shard_map/ppermute | solution.py:30
  128.1 2.6 %tile.2.refs_0_ = f32[2,896,896]{2,1,0:T(8,128)} custom-call(bf16[896,768]{1,0:T(8,128)(2,1)S(1)} %bitcast.17, bf16[768,896]{1,0:T(8,128)(2,1)S(1)} %bitcast.19), custom_call_target="tpu_custom_call" | custom-call | flops 1233125376 | bytes 5963776 | tf_op jit(solution)/shard_map/tile/pallas_call | solution.py:105
  130.7 0.2 collective-permute-done.6.right_ref
  130.8 2.5 %tile.3 = f32[2,896,896]{2,1,0:T(8,128)} custom-call(bf16[896,768]{1,0:T(8,128)(2,1)S(1)} %bitcast.18, bf16[768,896]{1,0:T(8,128)(2,1)S(1)} %collective-permute-done.6.right_ref, f32[2,896,896]{2,1,0:T(8,128)} %tile.2.refs_0_), custom_call_target="tpu_custom_call", output_to_operand_aliasing={{}: (2, {})} | custom-call | flops 1233125376 | bytes 5963776 | tf_op jit(solution)/shard_map/tile/pallas_call | solution.py:105
Async XLA Ops:
  0.6 13.3 %copy-start = (f32[1024]{0:T(1024)S(1)}, f32[1024]{0:T(1024)}, u32[]{:S(2)}) copy-start(f32[1024]{0:T(1024)} %param.5) | copy-start | bytes 12292
  53.0 28.4 %all-to-all-start.2 = ((bf16[8,96,896]{2,1,0:T(8,128)(2,1)}), bf16[8,96,896]{2,1,0:T(8,128)(2,1)S(1)}, u32[]{:S(2)}, u32[]{:S(2)}) async-start(bf16[8,96,896]{2,1,0:T(8,128)(2,1)} %broadcast_in_dim.16), calls=%async_computation.2 | async-start | bytes 2752512 | tf_op jit(solution)/shard_map/all_to_all | solution.py:21
  56.6 8.6 %collective-permute-start = (bf16[96,896]{1,0:T(8,128)(2,1)S(1)}, bf16[96,896]{1,0:T(8,128)(2,1)S(1)}, u32[]{:S(2)}, u32[]{:S(2)}) collective-permute-start(bf16[96,896]{1,0:T(8,128)(2,1)S(1)} %fusion.1.refs_0_), channel_id=1, source_target_pairs={{0,192},{32,224},{64,0},{96,32},{128,64},{160,96},{192,128},{224,1... | collective-permute-start | bytes 516104 | tf_op jit(solution)/shard_map/ppermute | solution.py:30
  65.2 7.8 %collective-permute-start.2 = (bf16[96,896]{1,0:T(8,128)(2,1)S(1)}, bf16[96,896]{1,0:T(8,128)(2,1)S(1)}, u32[]{:S(2)}, u32[]{:S(2)}) collective-permute-start(bf16[96,896]{1,0:T(8,128)(2,1)S(1)} %collective-permute-done.refs_2_), channel_id=1, source_target_pairs={{0,224},{32,0},{64,32},{96,64},{128,96},{160,128},{192,160},{224,1... | collective-permute-start | bytes 516104 | tf_op jit(solution)/shard_map/ppermute | solution.py:30
  70.5 5.8 %collective-permute-start.1 = (bf16[96,896]{1,0:T(8,128)(2,1)S(1)}, bf16[96,896]{1,0:T(8,128)(2,1)S(1)}, u32[]{:S(2)}, u32[]{:S(2)}) collective-permute-start(bf16[96,896]{1,0:T(8,128)(2,1)S(1)} %collective-permute-done.refs_2_), channel_id=1, source_target_pairs={{0,32},{32,64},{64,96},{96,128},{128,160},{160,192},{192,224},{224... | collective-permute-start | bytes 516104 | tf_op jit(solution)/shard_map/ppermute | solution.py:30
  73.0 6.8 %collective-permute-start.3 = (bf16[96,896]{1,0:T(8,128)(2,1)S(1)}, bf16[96,896]{1,0:T(8,128)(2,1)S(1)}, u32[]{:S(2)}, u32[]{:S(2)}) collective-permute-start(bf16[96,896]{1,0:T(8,128)(2,1)S(1)} %collective-permute-done.2.refs_3_), channel_id=1, source_target_pairs={{0,224},{32,0},{64,32},{96,64},{128,96},{160,128},{192,160},{224,1... | collective-permute-start | bytes 516104 | tf_op jit(solution)/shard_map/ppermute | solution.py:30
  81.4 35.8 %all-to-all-start.3 = ((bf16[16,96,896]{2,1,0:T(8,128)(2,1)}), bf16[16,96,896]{2,1,0:T(8,128)(2,1)}, u32[]{:S(2)}, u32[]{:S(2)}) async-start(bf16[16,96,896]{2,1,0:T(8,128)(2,1)} %slots.1), calls=%async_computation.3 | async-start | bytes 5505024 | tf_op jit(solution)/shard_map/all_to_all | solution.py:21
  88.5 10.5 %collective-permute-start.4 = (bf16[768,112]{1,0:T(8,128)(2,1)S(1)}, bf16[768,112]{1,0:T(8,128)(2,1)S(1)}, u32[]{:S(2)}, u32[]{:S(2)}) collective-permute-start(bf16[768,112]{1,0:T(8,128)(2,1)S(1)} %constant_dynamic-slice_fusion.2), channel_id=1, source_target_pairs={{0,128},{32,160},{64,192},{96,224},{128,0},{160,32},{192,64},{224,... | collective-permute-start | bytes 516104 | tf_op jit(solution)/shard_map/ppermute | solution.py:30
  99.4 9.6 %collective-permute-start.5 = (bf16[112,896]{1,0:T(8,128)(2,1)S(1)}, bf16[112,896]{1,0:T(8,128)(2,1)S(1)}, u32[]{:S(2)}, u32[]{:S(2)}) collective-permute-start(bf16[112,896]{1,0:T(8,128)(2,1)S(1)} %fusion), channel_id=1, source_target_pairs={{0,128},{32,160},{64,192},{96,224},{128,0},{160,32},{192,64},{224,... | collective-permute-start | bytes 602120 | tf_op jit(solution)/shard_map/ppermute | solution.py:30
  119.2 11.6 %collective-permute-start.6 = (bf16[768,896]{1,0:T(8,128)(2,1)S(1)}, bf16[768,896]{1,0:T(8,128)(2,1)S(1)}, u32[]{:S(2)}, u32[]{:S(2)}) collective-permute-start(bf16[768,896]{1,0:T(8,128)(2,1)S(1)} %bitcast.26), channel_id=1, source_target_pairs={{0,8},{8,0},{1,9},{9,1},{2,10},{10,2},{3,11},{11,3},{4,12},{12,4},... | collective-permute-start | bytes 4128776 | tf_op jit(solution)/shard_map/ppermute | solution.py:30
where the time goes:
time: 134 us
  blocking collectives  44.3 us (33%)
  starting transfers between devices  38.7 us (29%)
  waiting for transfers between devices  30.7 us (23%)
  Pallas kernels  13.1 us (10%)
  local copies, waits for them, and re-layouts  4.15 us (3%)
    all_to_all x2, blocking collectives, exchange(): return lax.all_to_all(pieces, axes, split_axis=0, concat_axis=0, tiled=True)  44.3 us
    ppermute x7, starting transfers between devices, passed_along(): lax.ppermute(shard, axis, [(i, (i + by) % devices) for i in range(devices)])  28.1 us
    ppermute x7, waiting for transfers between devices, passed_along(): lax.ppermute(shard, axis, [(i, (i + by) % devices) for i in range(devices)])  23.2 us
    all_to_all x2, starting transfers between devices, exchange(): return lax.all_to_all(pieces, axes, split_axis=0, concat_axis=0, tiled=True)  10.5 us
    all_to_all x2, waiting for transfers between devices, exchange(): return lax.all_to_all(pieces, axes, split_axis=0, concat_axis=0, tiled=True)  7.48 us
    pallas_call x2, Pallas kernels, tile_into(): pl.pallas_call(functools.partial(tile_kernel, place), in_specs=in_specs,...  5.09 us
    pallas_call x1, Pallas kernels, partial_sums(): pl.pallas_call(sums_kernel, in_specs=[pl.BlockSpec(memory_space=pltpu.VME...  3.81 us
  transfers between devices with their start and end apart: 9, of which 7 were waited for; matrix products, arithmetic and copies ran while one was open for 2% of the time, Pallas kernels for 3%

commit v1 on v0

--- a/solution.py
+++ b/solution.py
@@ -15,6 +15,7 @@
 PLANE = ("x", "yh", "yl")
 SLOTS_VMEM = 4 * 2**20
 TILE_VMEM = 16 * 2**20
+PIECES = ((0, 448), (448, 256), (704, 128), (832, 64))
 
 
 def exchange(pieces, axes):
@@ -77,26 +78,23 @@
 
 def tile_kernel(place, left_ref, right_ref, *refs):
     out_ref, rows_ref, sems = refs[-3:]
-    chunks, rows, _ = rows_ref.shape
     scale = 1.0 / right_ref.shape[0]
-
-    def copy(i):
-        return pltpu.make_async_copy(
-            rows_ref.at[i], out_ref.at[place, pl.ds(i * rows, rows)], sems.at[i]
+    copies = []
+    for i, (start, size) in enumerate(PIECES):
+        at = pl.ds(start, size)
+        left = left_ref[start : start + size, :]
+        product = jnp.dot(left, right_ref[...], preferred_element_type=jnp.float32)
+        rows_ref[at, :] = product * scale
+        copies.append(
+            pltpu.make_async_copy(rows_ref.at[at], out_ref.at[place, at], sems.at[i])
         )
-
-    for i in range(chunks):
-        left = left_ref[i * rows : (i + 1) * rows, :]
-        product = jnp.dot(left, right_ref[...], preferred_element_type=jnp.float32)
-        rows_ref[i] = product * scale
-        copy(i).start()
-    for i in range(chunks):
-        copy(i).wait()
-
-
-def tile_into(place, keys_t, partner, tiles=None, chunks=4):
+        copies[-1].start()
+    for copy in copies:
+        copy.wait()
+
+
+def tile_into(place, keys_t, partner, tiles=None):
     width, count = keys_t.shape
-    rows = width // chunks
     in_specs = [pl.BlockSpec(memory_space=pltpu.VMEM)] * 2
     args = [keys_t, partner]
     if tiles is not None:
@@ -108,8 +106,8 @@
         out_specs=pl.BlockSpec(memory_space=pltpu.HBM),
         out_shape=pltpu.HBM((2, width, width), jnp.float32),
         scratch_shapes=[
-            pltpu.VMEM((chunks, rows, width), jnp.float32),
-            pltpu.SemaphoreType.DMA((chunks,)),
+            pltpu.VMEM((width, width), jnp.float32),
+            pltpu.SemaphoreType.DMA((len(PIECES),)),
         ],
         input_output_aliases={} if tiles is None else {2: 0},
         cost_estimate=pl.CostEstimate(

time: 134 us -> 134 us (level)
  no operation moved by 1% of the time
where the time goes in v1:
time: 134 us
  blocking collectives  44.3 us (33%)
  starting transfers between devices  38.7 us (29%)
  waiting for transfers between devices  30.7 us (23%)
  Pallas kernels  13.2 us (10%)
  local copies, waits for them, and re-layouts  4.15 us (3%)
    all_to_all x2, blocking collectives, exchange(): return lax.all_to_all(pieces, axes, split_axis=0, concat_axis=0, tiled=True)  44.3 us
    ppermute x7, starting transfers between devices, passed_along(): lax.ppermute(shard, axis, [(i, (i + by) % devices) for i in range(devices)])  28.1 us
    ppermute x7, waiting for transfers between devices, passed_along(): lax.ppermute(shard, axis, [(i, (i + by) % devices) for i in range(devices)])  23.2 us
    all_to_all x2, starting transfers between devices, exchange(): return lax.all_to_all(pieces, axes, split_axis=0, concat_axis=0, tiled=True)  10.5 us
    all_to_all x2, waiting for transfers between devices, exchange(): return lax.all_to_all(pieces, axes, split_axis=0, concat_axis=0, tiled=True)  7.48 us
    pallas_call x2, Pallas kernels, tile_into(): pl.pallas_call(functools.partial(tile_kernel, place), in_specs=in_specs,...  5.19 us
    pallas_call x1, Pallas kernels, partial_sums(): pl.pallas_call(sums_kernel, in_specs=[pl.BlockSpec(memory_space=pltpu.VME...  3.81 us
  transfers between devices with their start and end apart: 9, of which 7 were waited for; matrix products, arithmetic and copies ran while one was open for 2% of the time, Pallas kernels for 3%

profile of v1, /device:TPU:1, one launch (start us, length us, event | category | flops | bytes accessed | tf_op | source)
XLA Modules:
  0.0 133.6 jit_solution(12244527188357441222)
XLA Ops:
  0.6 0.0 copy-start
  0.6 2.6 %fetch.1 = (f32[8,1,768]{2,1,0:T(1,128)S(1)}, bf16[768,1024]{1,0:T(8,128)(2,1)S(1)}, bf16[1024,896]{1,0:T(8,128)(2,1)S(1)}, bf16[1024,896]{1,0:T(8,128)(2,1)S(1)}) custom-call(bf16[768,1024]{1,0:T(8,128)(2,1)} %states_in.1, bf16[1024,896]{1,0:T(8,128)(2,1)} %gate_in.1, bf16[1024,896]{1,0:T(8,128)(2,1)} %up_in.1), custom_call_target="tpu_custom_call" | custom-call | flops 1572864 | bytes 5242880 | tf_op jit(solution)/shard_map/fetch/pallas_call | solution.py:140
  3.2 10.7 %all_to_all.20.squares_ref = f32[8,1,768]{2,1,0:T(1,128)S(1)} all-to-all(f32[8,1,768]{2,1,0:T(1,128)S(1)} %get-tuple-element.12), channel_id=1, replica_groups=mesh['z'=8,'yh'=2,'k'=2,'x'=4,'yl'=2] {'x','yl'}, dimensions={0} | all-to-all | bytes 49152 | tf_op jit(solution)/shard_map/all_to_all | solution.py:22
  13.9 0.0 copy-done
  13.9 3.8 %sums.1 = bf16[768,1792]{1,0:T(8,128)(2,1)S(1)} custom-call(bf16[768,1024]{1,0:T(8,128)(2,1)S(1)} %get-tuple-element.11.states_ref, f32[8,1,768]{2,1,0:T(1,128)S(1)} %all_to_all.20.squares_ref, f32[1,1024]{1,0:T(1,128)S(1)} %bitcast.21, bf16[1024,896]{1,0:T(8,128)(2,1)S(1)} %get-tuple-element.13.gate_ref, bf16[1024,896]{1,0:T(8,128)(2,1)S(1)} %get-tuple-element.14.up_ref), custom_call_target="tpu_custom_call" | custom-call | flops 2818572288 | bytes 7995392 | tf_op jit(solution)/shard_map/sums/pallas_call | solution.py:175
  17.7 33.6 %all_to_all.21 = bf16[8,96,1792]{2,1,0:T(8,128)(2,1)S(1)} all-to-all(bf16[8,96,1792]{2,1,0:T(8,128)(2,1)S(1)} %bitcast.20), channel_id=1, replica_groups=mesh['z'=8,'yh'=2,'k'=2,'x'=4,'yl'=2] {'x','yl'}, dimensions={0} | all-to-all | bytes 5505024 | tf_op jit(solution)/shard_map/all_to_all | solution.py:22
  51.3 0.4 convert_reduce_fusion
  51.7 0.1 fusion.1.refs_0_
  51.8 1.2 broadcast_in_dim.16
  53.0 3.6 %all-to-all-start.2 = ((bf16[8,96,896]{2,1,0:T(8,128)(2,1)}), bf16[8,96,896]{2,1,0:T(8,128)(2,1)S(1)}, u32[]{:S(2)}, u32[]{:S(2)}) async-start(bf16[8,96,896]{2,1,0:T(8,128)(2,1)} %broadcast_in_dim.16), calls=%async_computation.2 | async-start | bytes 2752512 | tf_op jit(solution)/shard_map/all_to_all | solution.py:22
  56.6 6.1 %collective-permute-start = (bf16[96,896]{1,0:T(8,128)(2,1)S(1)}, bf16[96,896]{1,0:T(8,128)(2,1)S(1)}, u32[]{:S(2)}, u32[]{:S(2)}) collective-permute-start(bf16[96,896]{1,0:T(8,128)(2,1)S(1)} %fusion.1.refs_0_), channel_id=1, source_target_pairs={{0,192},{32,224},{64,0},{96,32},{128,64},{160,96},{192,128},{224,1... | collective-permute-start | bytes 516104 | tf_op jit(solution)/shard_map/ppermute | solution.py:31
  62.7 2.5 %collective-permute-done.refs_2_ = bf16[96,896]{1,0:T(8,128)(2,1)S(1)} collective-permute-done((bf16[96,896]{1,0:T(8,128)(2,1)S(1)}, bf16[96,896]{1,0:T(8,128)(2,1)S(1)}, u32[]{:S(2)}, u32[]{:S(2)}) %collective-permute-start) | collective-permute-done | bytes 172064 | tf_op jit(solution)/shard_map/ppermute | solution.py:31
  65.2 5.3 %collective-permute-start.2 = (bf16[96,896]{1,0:T(8,128)(2,1)S(1)}, bf16[96,896]{1,0:T(8,128)(2,1)S(1)}, u32[]{:S(2)}, u32[]{:S(2)}) collective-permute-start(bf16[96,896]{1,0:T(8,128)(2,1)S(1)} %collective-permute-done.refs_2_), channel_id=1, source_target_pairs={{0,224},{32,0},{64,32},{96,64},{128,96},{160,128},{192,160},{224,1... | collective-permute-start | bytes 516104 | tf_op jit(solution)/shard_map/ppermute | solution.py:31
  70.5 0.0 collective-permute-start.1
  70.5 2.5 %collective-permute-done.2.refs_3_ = bf16[96,896]{1,0:T(8,128)(2,1)S(1)} collective-permute-done((bf16[96,896]{1,0:T(8,128)(2,1)S(1)}, bf16[96,896]{1,0:T(8,128)(2,1)S(1)}, u32[]{:S(2)}, u32[]{:S(2)}) %collective-permute-start.2) | collective-permute-done | bytes 172064 | tf_op jit(solution)/shard_map/ppermute | solution.py:31
  73.0 3.3 %collective-permute-start.3 = (bf16[96,896]{1,0:T(8,128)(2,1)S(1)}, bf16[96,896]{1,0:T(8,128)(2,1)S(1)}, u32[]{:S(2)}, u32[]{:S(2)}) collective-permute-start(bf16[96,896]{1,0:T(8,128)(2,1)S(1)} %collective-permute-done.2.refs_3_), channel_id=1, source_target_pairs={{0,224},{32,0},{64,32},{96,64},{128,96},{160,128},{192,160},{224,1... | collective-permute-start | bytes 516104 | tf_op jit(solution)/shard_map/ppermute | solution.py:31
  76.3 0.0 collective-permute-done.1.refs_1_
  76.3 3.5 %collective-permute-done.3.refs_4_ = bf16[96,896]{1,0:T(8,128)(2,1)S(1)} collective-permute-done((bf16[96,896]{1,0:T(8,128)(2,1)S(1)}, bf16[96,896]{1,0:T(8,128)(2,1)S(1)}, u32[]{:S(2)}, u32[]{:S(2)}) %collective-permute-start.3) | collective-permute-done | bytes 172064 | tf_op jit(solution)/shard_map/ppermute | solution.py:31
  79.7 1.7 %slots.1 = bf16[16,96,896]{2,1,0:T(8,128)(2,1)} custom-call(bf16[96,896]{1,0:T(8,128)(2,1)S(1)} %fusion.1.refs_0_, bf16[96,896]{1,0:T(8,128)(2,1)S(1)} %collective-permute-done.1.refs_1_, bf16[96,896]{1,0:T(8,128)(2,1)S(1)} %collective-permute-done.refs_2_, bf16[96,896]{1,0:T(8,128)(2,1)S(1)} %collective-permute-done.2.refs_3_, ...), custom_call_target="tpu_custom_call" | custom-call | flops 1376256 | bytes 3612672 | tf_op jit(solution)/shard_map/slots/pallas_call | solution.py:65
  81.4 0.0 all-to-all-done.2
  81.4 7.0 %all-to-all-start.3 = ((bf16[16,96,896]{2,1,0:T(8,128)(2,1)}), bf16[16,96,896]{2,1,0:T(8,128)(2,1)}, u32[]{:S(2)}, u32[]{:S(2)}) async-start(bf16[16,96,896]{2,1,0:T(8,128)(2,1)} %slots.1), calls=%async_computation.3 | async-start | bytes 5505024 | tf_op jit(solution)/shard_map/all_to_all | solution.py:22
  88.4 0.1 constant_dynamic-slice_fusion.2
  88.5 2.5 %collective-permute-start.4 = (bf16[768,112]{1,0:T(8,128)(2,1)S(1)}, bf16[768,112]{1,0:T(8,128)(2,1)S(1)}, u32[]{:S(2)}, u32[]{:S(2)}) collective-permute-start(bf16[768,112]{1,0:T(8,128)(2,1)S(1)} %constant_dynamic-slice_fusion.2), channel_id=1, source_target_pairs={{0,128},{32,160},{64,192},{96,224},{128,0},{160,32},{192,64},{224,... | collective-permute-start | bytes 516104 | tf_op jit(solution)/shard_map/ppermute | solution.py:31
  91.0 8.0 %collective-permute-done.4 = bf16[768,112]{1,0:T(8,128)(2,1)S(1)} collective-permute-done((bf16[768,112]{1,0:T(8,128)(2,1)S(1)}, bf16[768,112]{1,0:T(8,128)(2,1)S(1)}, u32[]{:S(2)}, u32[]{:S(2)}) %collective-permute-start.4) | collective-permute-done | bytes 172064 | tf_op jit(solution)/shard_map/ppermute | solution.py:31
  99.0 0.4 fusion
  99.4 2.1 %collective-permute-start.5 = (bf16[112,896]{1,0:T(8,128)(2,1)S(1)}, bf16[112,896]{1,0:T(8,128)(2,1)S(1)}, u32[]{:S(2)}, u32[]{:S(2)}) collective-permute-start(bf16[112,896]{1,0:T(8,128)(2,1)S(1)} %fusion), channel_id=1, source_target_pairs={{0,128},{32,160},{64,192},{96,224},{128,0},{160,32},{192,64},{224,... | collective-permute-start | bytes 602120 | tf_op jit(solution)/shard_map/ppermute | solution.py:31
  101.5 0.9 copy.10
  102.3 6.6 %collective-permute-done.5 = bf16[112,896]{1,0:T(8,128)(2,1)S(1)} collective-permute-done((bf16[112,896]{1,0:T(8,128)(2,1)S(1)}, bf16[112,896]{1,0:T(8,128)(2,1)S(1)}, u32[]{:S(2)}, u32[]{:S(2)}) %collective-permute-start.5) | collective-permute-done | bytes 200736 | tf_op jit(solution)/shard_map/ppermute | solution.py:31
  109.0 0.8 bitcast_convert_fusion
  109.7 7.5 %all-to-all-done.3 = bf16[16,96,896]{2,1,0:T(8,128)(2,1)} async-done(((bf16[16,96,896]{2,1,0:T(8,128)(2,1)}), bf16[16,96,896]{2,1,0:T(8,128)(2,1)}, u32[]{:S(2)}, u32[]{:S(2)}) %all-to-all-start.3) | async-done | bytes 2752544 | tf_op jit(solution)/shard_map/all_to_all | solution.py:22
  117.2 2.0 %constant_dynamic-slice_fusion = (bf16[4,1,2,96,896]{4,3,2,1,0:T(8,128)(2,1)S(1)}, bf16[4,1,2,96,896]{4,3,2,1,0:T(8,128)(2,1)S(1)}) fusion(bf16[4,2,2,96,896]{4,3,2,1,0:T(8,128)(2,1)} %bitcast.5, s32[]{:T(128)S(6)} %select_n.17, s32[]{:T(128)S(6)} %select_n.16), kind=kLoop, calls=%fused_computation.6 | loop fusion | bytes 5505032 | tf_op jit(solution)/shard_map/jit(dynamic_index_in_dim)/dynamic_slice | solution.py:226
  119.2 8.9 %collective-permute-start.6 = (bf16[768,896]{1,0:T(8,128)(2,1)S(1)}, bf16[768,896]{1,0:T(8,128)(2,1)S(1)}, u32[]{:S(2)}, u32[]{:S(2)}) collective-permute-start(bf16[768,896]{1,0:T(8,128)(2,1)S(1)} %bitcast.26), channel_id=1, source_target_pairs={{0,8},{8,0},{1,9},{9,1},{2,10},{10,2},{3,11},{11,3},{4,12},{12,4},... | collective-permute-start | bytes 4128776 | tf_op jit(solution)/shard_map/ppermute | solution.py:31
  128.1 2.6 %tile.2.refs_0_ = f32[2,896,896]{2,1,0:T(8,128)} custom-call(bf16[896,768]{1,0:T(8,128)(2,1)S(1)} %bitcast.17, bf16[768,896]{1,0:T(8,128)(2,1)S(1)} %bitcast.19), custom_call_target="tpu_custom_call" | custom-call | flops 1233125376 | bytes 5963776 | tf_op jit(solution)/shard_map/tile/pallas_call | solution.py:103
  130.7 0.1 collective-permute-done.6.right_ref
  130.8 2.6 %tile.3 = f32[2,896,896]{2,1,0:T(8,128)} custom-call(bf16[896,768]{1,0:T(8,128)(2,1)S(1)} %bitcast.18, bf16[768,896]{1,0:T(8,128)(2,1)S(1)} %collective-permute-done.6.right_ref, f32[2,896,896]{2,1,0:T(8,128)} %tile.2.refs_0_), custom_call_target="tpu_custom_call", output_to_operand_aliasing={{}: (2, {})} | custom-call | flops 1233125376 | bytes 5963776 | tf_op jit(solution)/shard_map/tile/pallas_call | solution.py:103
Async XLA Ops:
  0.6 13.3 %copy-start = (f32[1024]{0:T(1024)S(1)}, f32[1024]{0:T(1024)}, u32[]{:S(2)}) copy-start(f32[1024]{0:T(1024)} %param.5) | copy-start | bytes 12292
  53.0 28.4 %all-to-all-start.2 = ((bf16[8,96,896]{2,1,0:T(8,128)(2,1)}), bf16[8,96,896]{2,1,0:T(8,128)(2,1)S(1)}, u32[]{:S(2)}, u32[]{:S(2)}) async-start(bf16[8,96,896]{2,1,0:T(8,128)(2,1)} %broadcast_in_dim.16), calls=%async_computation.2 | async-start | bytes 2752512 | tf_op jit(solution)/shard_map/all_to_all | solution.py:22
  56.6 8.6 %collective-permute-start = (bf16[96,896]{1,0:T(8,128)(2,1)S(1)}, bf16[96,896]{1,0:T(8,128)(2,1)S(1)}, u32[]{:S(2)}, u32[]{:S(2)}) collective-permute-start(bf16[96,896]{1,0:T(8,128)(2,1)S(1)} %fusion.1.refs_0_), channel_id=1, source_target_pairs={{0,192},{32,224},{64,0},{96,32},{128,64},{160,96},{192,128},{224,1... | collective-permute-start | bytes 516104 | tf_op jit(solution)/shard_map/ppermute | solution.py:31
  65.2 7.8 %collective-permute-start.2 = (bf16[96,896]{1,0:T(8,128)(2,1)S(1)}, bf16[96,896]{1,0:T(8,128)(2,1)S(1)}, u32[]{:S(2)}, u32[]{:S(2)}) collective-permute-start(bf16[96,896]{1,0:T(8,128)(2,1)S(1)} %collective-permute-done.refs_2_), channel_id=1, source_target_pairs={{0,224},{32,0},{64,32},{96,64},{128,96},{160,128},{192,160},{224,1... | collective-permute-start | bytes 516104 | tf_op jit(solution)/shard_map/ppermute | solution.py:31
  70.5 5.8 %collective-permute-start.1 = (bf16[96,896]{1,0:T(8,128)(2,1)S(1)}, bf16[96,896]{1,0:T(8,128)(2,1)S(1)}, u32[]{:S(2)}, u32[]{:S(2)}) collective-permute-start(bf16[96,896]{1,0:T(8,128)(2,1)S(1)} %collective-permute-done.refs_2_), channel_id=1, source_target_pairs={{0,32},{32,64},{64,96},{96,128},{128,160},{160,192},{192,224},{224... | collective-permute-start | bytes 516104 | tf_op jit(solution)/shard_map/ppermute | solution.py:31
  73.0 6.8 %collective-permute-start.3 = (bf16[96,896]{1,0:T(8,128)(2,1)S(1)}, bf16[96,896]{1,0:T(8,128)(2,1)S(1)}, u32[]{:S(2)}, u32[]{:S(2)}) collective-permute-start(bf16[96,896]{1,0:T(8,128)(2,1)S(1)} %collective-permute-done.2.refs_3_), channel_id=1, source_target_pairs={{0,224},{32,0},{64,32},{96,64},{128,96},{160,128},{192,160},{224,1... | collective-permute-start | bytes 516104 | tf_op jit(solution)/shard_map/ppermute | solution.py:31
  81.4 35.8 %all-to-all-start.3 = ((bf16[16,96,896]{2,1,0:T(8,128)(2,1)}), bf16[16,96,896]{2,1,0:T(8,128)(2,1)}, u32[]{:S(2)}, u32[]{:S(2)}) async-start(bf16[16,96,896]{2,1,0:T(8,128)(2,1)} %slots.1), calls=%async_computation.3 | async-start | bytes 5505024 | tf_op jit(solution)/shard_map/all_to_all | solution.py:22
  88.5 10.5 %collective-permute-start.4 = (bf16[768,112]{1,0:T(8,128)(2,1)S(1)}, bf16[768,112]{1,0:T(8,128)(2,1)S(1)}, u32[]{:S(2)}, u32[]{:S(2)}) collective-permute-start(bf16[768,112]{1,0:T(8,128)(2,1)S(1)} %constant_dynamic-slice_fusion.2), channel_id=1, source_target_pairs={{0,128},{32,160},{64,192},{96,224},{128,0},{160,32},{192,64},{224,... | collective-permute-start | bytes 516104 | tf_op jit(solution)/shard_map/ppermute | solution.py:31
  99.4 9.6 %collective-permute-start.5 = (bf16[112,896]{1,0:T(8,128)(2,1)S(1)}, bf16[112,896]{1,0:T(8,128)(2,1)S(1)}, u32[]{:S(2)}, u32[]{:S(2)}) collective-permute-start(bf16[112,896]{1,0:T(8,128)(2,1)S(1)} %fusion), channel_id=1, source_target_pairs={{0,128},{32,160},{64,192},{96,224},{128,0},{160,32},{192,64},{224,... | collective-permute-start | bytes 602120 | tf_op jit(solution)/shard_map/ppermute | solution.py:31
  119.2 11.6 %collective-permute-start.6 = (bf16[768,896]{1,0:T(8,128)(2,1)S(1)}, bf16[768,896]{1,0:T(8,128)(2,1)S(1)}, u32[]{:S(2)}, u32[]{:S(2)}) collective-permute-start(bf16[768,896]{1,0:T(8,128)(2,1)S(1)} %bitcast.26), channel_id=1, source_target_pairs={{0,8},{8,0},{1,9},{9,1},{2,10},{10,2},{3,11},{11,3},{4,12},{12,4},... | collective-permute-start | bytes 4128776 | tf_op jit(solution)/shard_map/ppermute | solution.py:31
